TPU v7x, 32 devices: a whole 2x2x4 slice. The times are simulated.
32 devices in a mesh: gx: 4 (over y, x), gy: 4 (over z), gz: 2 (over core).
Axes of the slice: x: 2, y: 2, z: 4, core: 2. Of those that a mesh axis runs over, the one named last changes fastest.
Arguments:
- residual: float32 [3, 32, 256, 512], P(None, 'gz', 'gx', 'gy'), may hold values from -32 to 32
- edge_diag: float32 [3, 32, 256, 512], P(None, 'gz', 'gx', 'gy'), may hold values from 6.5 to 9
- node_shift: float32 [32, 256, 512], P('gz', 'gx', 'gy'), may hold values from 0.05 to 3
- coarse_shift: float32 [16, 128, 256], P('gz', 'gx', 'gy'), may hold values from 0.05 to 3
Outputs:
- correction: float32 [3, 32, 256, 512], P(None, 'gz', 'gx', 'gy')
All inputs are finite; a program needn't handle non-finite values.
Results may differ from a plain program's by a relative error of at most 0.000021.
Values sent between devices are 32-bit elements; how exact they have to be, the bound alone decides.
A program may use at most 128 MiB of HBM per device.

v0:
```python
import jax
import jax.numpy as jnp
from jax import lax
from jax.sharding import PartitionSpec as P


def with_halo(block, sides, width):
    for axis, dim in sides:
        count = lax.axis_size(axis)
        forward = [(i, i + 1) for i in range(count - 1)]
        backward = [(target, source) for source, target in forward]
        low = lax.ppermute(
            lax.slice_in_dim(block, block.shape[dim] - width, None, axis=dim), axis, forward
        )
        high = lax.ppermute(lax.slice_in_dim(block, 0, width, axis=dim), axis, backward)
        block = jnp.concatenate([low, block, high], axis=dim)
    return block


def neighbours(padded):
    total = padded[2:, 1:-1, 1:-1] + padded[:-2, 1:-1, 1:-1]
    total = total + padded[1:-1, 2:, 1:-1] + padded[1:-1, :-2, 1:-1]
    return total + padded[1:-1, 1:-1, 2:] + padded[1:-1, 1:-1, :-2]


def node_faces(field):
    return with_halo(field, (("gx", 1), ("gy", 2), ("gz", 0)), 1)


def coarse_faces(field):
    return with_halo(field, (("gx", 1), ("gy", 2), ("gz", 0)), 1)


def apply_padded(padded, diagonal):
    return diagonal * padded[1:-1, 1:-1, 1:-1] - neighbours(padded)


def local(residual, edge_diag, node_shift, coarse_shift):
    joined = jnp.concatenate((residual, edge_diag), axis=0)
    padded_both = with_halo(joined, (("gx", 2), ("gy", 3), ("gz", 1)), 1)
    padded_diag = padded_both[3:]
    padded = padded_both[:3] / jnp.where(padded_diag > 0.0, padded_diag, 1.0)
    scaled = padded[:, 1:-1, 1:-1, 1:-1]
    edge_near = jnp.stack([neighbours(padded[component]) for component in range(3)])
    smooth_part = 2.0 * scaled - (edge_diag * scaled - edge_near) / edge_diag
    nodal_rhs = (
        padded[0, :-2, 1:-1, 1:-1]
        - scaled[0]
        + (padded[1, 1:-1, :-2, 1:-1] - scaled[1])
        + (padded[2, 1:-1, 1:-1, :-2] - scaled[2])
    )
    node_diag = 6.0 + node_shift
    first_guess = nodal_rhs / node_diag
    node_res = nodal_rhs - apply_padded(node_faces(first_guess), node_diag)
    sx, sy, sz = node_res.shape
    coarse_rhs = node_res.reshape(sx // 2, 2, sy // 2, 2, sz // 2, 2).sum(axis=(1, 3, 5))
    coarse_diag = 6.0 + coarse_shift
    first_dir = coarse_rhs / coarse_diag
    first_image = apply_padded(coarse_faces(first_dir), coarse_diag)
    second_dir = first_image / coarse_diag
    second_image = apply_padded(coarse_faces(second_dir), coarse_diag)
    gone, gtwo, hone, hmix, htwo = lax.psum(
        (
            jnp.sum(first_dir * coarse_rhs),
            jnp.sum(second_dir * coarse_rhs),
            jnp.sum(first_dir * first_image),
            jnp.sum(second_dir * first_image),
            jnp.sum(second_dir * second_image),
        ),
        ("gx", "gy", "gz"),
    )
    coef_two = (gtwo - hmix * gone / hone) / (htwo - hmix * hmix / hone)
    coef_one = (gone - hmix * coef_two) / hone
    coarse_sol = coef_one * first_dir + coef_two * second_dir
    spread = jnp.broadcast_to(
        coarse_sol[:, None, :, None, :, None], (sx // 2, 2, sy // 2, 2, sz // 2, 2)
    ).reshape(sx, sy, sz)
    nodal = first_guess + spread
    final_nodal = nodal + (nodal_rhs - apply_padded(node_faces(nodal), node_diag)) / node_diag
    fpad = node_faces(final_nodal)
    grads = jnp.stack(
        [
            fpad[2:, 1:-1, 1:-1] - final_nodal,
            fpad[1:-1, 2:, 1:-1] - final_nodal,
            fpad[1:-1, 1:-1, 2:] - final_nodal,
        ]
    )
    return smooth_part + grads


def solution(mesh):
    placed = (
        P(None, "gz", "gx", "gy"),
        P(None, "gz", "gx", "gy"),
        P("gz", "gx", "gy"),
        P("gz", "gx", "gy"),
    )
    return jax.shard_map(
        local, mesh=mesh, in_specs=placed, out_specs=P(None, "gz", "gx", "gy"), check_vma=False
    )
```

profile of v0, /device:TPU:0, one launch (start us, length us, event | category | flops | bytes accessed | tf_op | source)
XLA Modules:
  0.0 311.6 jit_solution(5837893788152960340)
XLA Ops:
  2.1 4.9 %collective-permute-start = (f32[6,16,1,128]{3,2,1,0:T(1,128)S(1)}, f32[6,16,1,128]{3,2,1,0:T(1,128)S(1)}, u32[]{:S(2)}, u32[]{:S(2)}) collective-permute-start(f32[6,16,1,128]{3,2,1,0:T(1,128)S(1)} %get-tuple-element.24), channel_id=1, source_target_pairs={{0,8},{8,16},{16,24},{1,9},{9,17},{17,25},{2,10},{10,18},{18,26},{... | collective-permute-start | bytes 147464 | tf_op jit(solution)/shard_map/ppermute | solution.py:12
  8.8 4.3 %collective-permute-done.1 = f32[6,16,1,128]{3,2,1,0:T(1,128)S(1)} collective-permute-done((f32[6,16,1,128]{3,2,1,0:T(1,128)S(1)}, f32[6,16,1,128]{3,2,1,0:T(1,128)S(1)}, u32[]{:S(2)}, u32[]{:S(2)}) %collective-permute-start.1) | collective-permute-done | bytes 49184 | tf_op jit(solution)/shard_map/ppermute | solution.py:15
  13.6 4.0 %fusion.47 = (f32[6,16,66,1]{3,2,1,0:T(8,128)}, f32[6,16,66,1]{3,2,1,0:T(8,128)}) fusion(f32[6,16,66,128]{3,2,1,0:T(8,128)S(1)} %pad_maximum_fusion.1), kind=kLoop, calls=%fused_computation.196 | loop fusion | bytes 101376 | tf_op jit(solution)/shard_map/slice | solution.py:13
  20.2 3.5 %collective-permute-start.2 = (f32[6,16,66,1]{2,1,3,0:T(8,128)S(1)}, f32[6,16,66,1]{2,1,3,0:T(8,128)S(1)}, u32[]{:S(2)}, u32[]{:S(2)}) collective-permute-start(f32[6,16,66,1]{2,1,3,0:T(8,128)S(1)} %copy.5), channel_id=1, source_target_pairs={{0,2},{2,4},{4,6},{1,3},{3,5},{5,7},{8,10},{10,12},{12,14},{9,11},... | collective-permute-start | bytes 76040 | tf_op jit(solution)/shard_map/ppermute | solution.py:12
  42.0 5.0 %pad_maximum_fusion = f32[6,18,66,130]{3,2,1,0:T(8,128)S(1)} fusion(f32[6,1,66,130]{3,2,1,0:T(8,128)S(1)} %collective-permute-done.5, f32[6,16,66,1]{3,2,1,0:T(8,128)S(1)} %copy-done.3, f32[6,16,1,128]{3,2,1,0:T(1,128)S(1)} %collective-permute-done.1, f32[6,16,64,128]{3,2,1,0:T(8,128)S(1)} %constant_dynamic-update-slice_fusion, ...), kind=kLoop, calls=%fused_computation.1 | loop fusion | flops 5559840 | bytes 7413120 | tf_op jit(solution)/shard_map/concatenate | solution.py:16
  48.8 4.3 %collective-permute-start.6 = (f32[16,1,128]{2,1,0:T(1,128)S(1)}, f32[16,1,128]{2,1,0:T(1,128)S(1)}, u32[]{:S(2)}, u32[]{:S(2)}) collective-permute-start(f32[16,1,128]{2,1,0:T(1,128)S(1)} %get-tuple-element.43), channel_id=1, source_target_pairs={{0,8},{8,16},{16,24},{1,9},{9,17},{17,25},{2,10},{10,18},{18,26},{... | collective-permute-start | bytes 24584 | tf_op jit(solution)/shard_map/ppermute | solution.py:12
  54.5 4.2 %collective-permute-done.7 = f32[16,1,128]{2,1,0:T(1,128)S(1)} collective-permute-done((f32[16,1,128]{2,1,0:T(1,128)S(1)}, f32[16,1,128]{2,1,0:T(1,128)S(1)}, u32[]{:S(2)}, u32[]{:S(2)}) %collective-permute-start.7) | collective-permute-done | bytes 8224 | tf_op jit(solution)/shard_map/ppermute | solution.py:15
  64.6 3.9 %collective-permute-done.9 = f32[16,66,1]{1,0,2:T(8,128)S(1)} collective-permute-done((f32[16,66,1]{1,0,2:T(8,128)S(1)}, f32[16,66,1]{1,0,2:T(8,128)S(1)}, u32[]{:S(2)}, u32[]{:S(2)}) %collective-permute-start.9) | collective-permute-done | bytes 4256 | tf_op jit(solution)/shard_map/ppermute | solution.py:15
  75.0 34.9 %reshape.12 = f32[8,2,32,2,64,2]{5,4,3,2,1,0:T(8,128)} reshape(f32[16,64,128]{2,1,0:T(8,128)S(1)} %fusion.21) | data formatting | bytes 1048576 | tf_op jit(solution)/shard_map/reshape | solution.py:56
  109.8 12.2 %reduce_sum.54 = f32[8,32,64]{2,1,0:T(8,128)S(1)} reduce(f32[8,2,32,2,64,2]{5,4,3,2,1,0:T(8,128)} %reshape.12, f32[]{:T(128)} %constant.4.clone.1), dimensions={1,3,5}, to_apply=%region_0.1 | reduce | flops 114688 | bytes 589828 | tf_op jit(solution)/shard_map/reduce_sum | solution.py:56
  126.9 4.2 %collective-permute-done.13 = f32[8,1,64]{2,1,0:T(1,128)S(1)} collective-permute-done((f32[8,1,64]{2,1,0:T(1,128)S(1)}, f32[8,1,64]{2,1,0:T(1,128)S(1)}, u32[]{:S(2)}, u32[]{:S(2)}) %collective-permute-start.13) | collective-permute-done | bytes 2080 | tf_op jit(solution)/shard_map/ppermute | solution.py:15
  131.2 3.5 %collective-permute-start.14 = (f32[8,34,1]{2,1,0:T(8,128)S(1)}, f32[8,34,1]{2,1,0:T(8,128)S(1)}, u32[]{:S(2)}, u32[]{:S(2)}) collective-permute-start(f32[8,34,1]{2,1,0:T(8,128)S(1)} %get-tuple-element.52), channel_id=1, source_target_pairs={{0,2},{2,4},{4,6},{1,3},{3,5},{5,7},{8,10},{10,12},{12,14},{9,11},... | collective-permute-start | bytes 3272 | tf_op jit(solution)/shard_map/ppermute | solution.py:12
  137.5 4.4 %collective-permute-done.15 = f32[8,34,1]{2,1,0:T(8,128)S(1)} collective-permute-done((f32[8,34,1]{2,1,0:T(8,128)S(1)}, f32[8,34,1]{2,1,0:T(8,128)S(1)}, u32[]{:S(2)}, u32[]{:S(2)}) %collective-permute-start.15) | collective-permute-done | bytes 1120 | tf_op jit(solution)/shard_map/ppermute | solution.py:15
  152.3 4.2 %collective-permute-done.19 = f32[8,1,64]{2,1,0:T(1,128)S(1)} collective-permute-done((f32[8,1,64]{2,1,0:T(1,128)S(1)}, f32[8,1,64]{2,1,0:T(1,128)S(1)}, u32[]{:S(2)}, u32[]{:S(2)}) %collective-permute-start.19) | collective-permute-done | bytes 2080 | tf_op jit(solution)/shard_map/ppermute | solution.py:15
  162.1 4.4 %collective-permute-done.21 = f32[8,34,1]{2,1,0:T(8,128)S(1)} collective-permute-done((f32[8,34,1]{2,1,0:T(8,128)S(1)}, f32[8,34,1]{2,1,0:T(8,128)S(1)}, u32[]{:S(2)}, u32[]{:S(2)}) %collective-permute-start.21) | collective-permute-done | bytes 1120 | tf_op jit(solution)/shard_map/ppermute | solution.py:15
  172.7 38.0 %all-reduce = (f32[]{:T(128)}, f32[]{:T(128)}, f32[]{:T(128)}, f32[]{:T(128)}, f32[]{:T(128)}) all-reduce(f32[]{:T(128)} %get-tuple-element.7, f32[]{:T(128)} %get-tuple-element.6, f32[]{:T(128)} %get-tuple-element.8, f32[]{:T(128)} %get-tuple-element.5, f32[]{:T(128)} %fusion.35), channel_id=1, replica_groups=mesh['gx'=4,'gy'=4,'gz'=2] {'gx','gy','gz'}, use_global_device_ids=true, to_apply=%region_6.7 | all-reduce | flops 5 | bytes 40 | tf_op jit(solution)/shard_map/psum | solution.py:62
  217.8 11.4 %broadcast_in_dim.11 = f32[8,2,32,2,64,2]{5,4,3,2,1,0:T(8,128)} broadcast(f32[8,32,64]{2,1,0:T(8,128)S(1)} %multiply_add_fusion), dimensions={0,2,4} | broadcast | bytes 589824 | tf_op jit(solution)/shard_map/broadcast_in_dim | solution.py:75
  229.2 24.0 %reshape.13 = f32[16,64,128]{2,1,0:T(8,128)S(1)} reshape(f32[8,2,32,2,64,2]{5,4,3,2,1,0:T(8,128)} %broadcast_in_dim.11) | data formatting | bytes 1048576 | tf_op jit(solution)/shard_map/reshape | solution.py:77
  253.4 4.2 %collective-permute-start.24 = (f32[16,1,128]{2,1,0:T(1,128)S(1)}, f32[16,1,128]{2,1,0:T(1,128)S(1)}, u32[]{:S(2)}, u32[]{:S(2)}) collective-permute-start(f32[16,1,128]{2,1,0:T(1,128)S(1)} %get-tuple-element.41), channel_id=1, source_target_pairs={{0,8},{8,16},{16,24},{1,9},{9,17},{17,25},{2,10},{10,18},{18,26},{... | collective-permute-start | bytes 24584 | tf_op jit(solution)/shard_map/ppermute | solution.py:12
  258.9 4.2 %collective-permute-done.25 = f32[16,1,128]{2,1,0:T(1,128)S(1)} collective-permute-done((f32[16,1,128]{2,1,0:T(1,128)S(1)}, f32[16,1,128]{2,1,0:T(1,128)S(1)}, u32[]{:S(2)}, u32[]{:S(2)}) %collective-permute-start.25) | collective-permute-done | bytes 8224 | tf_op jit(solution)/shard_map/ppermute | solution.py:15
  263.6 4.0 %collective-permute-start.26 = (f32[16,66,1]{1,0,2:T(8,128)S(1)}, f32[16,66,1]{1,0,2:T(8,128)S(1)}, u32[]{:S(2)}, u32[]{:S(2)}) collective-permute-start(f32[16,66,1]{1,0,2:T(8,128)S(1)} %copy.15), channel_id=1, source_target_pairs={{0,2},{2,4},{4,6},{1,3},{3,5},{5,7},{8,10},{10,12},{12,14},{9,11},... | collective-permute-start | bytes 12680 | tf_op jit(solution)/shard_map/ppermute | solution.py:12
  269.5 3.9 %collective-permute-done.27 = f32[16,66,1]{1,0,2:T(8,128)S(1)} collective-permute-done((f32[16,66,1]{1,0,2:T(8,128)S(1)}, f32[16,66,1]{1,0,2:T(8,128)S(1)}, u32[]{:S(2)}, u32[]{:S(2)}) %collective-permute-start.27) | collective-permute-done | bytes 4256 | tf_op jit(solution)/shard_map/ppermute | solution.py:15
  281.2 4.5 %collective-permute-start.30 = (f32[16,1,128]{2,1,0:T(1,128)S(1)}, f32[16,1,128]{2,1,0:T(1,128)S(1)}, u32[]{:S(2)}, u32[]{:S(2)}) collective-permute-start(f32[16,1,128]{2,1,0:T(1,128)S(1)} %get-tuple-element.39), channel_id=1, source_target_pairs={{0,8},{8,16},{16,24},{1,9},{9,17},{17,25},{2,10},{10,18},{18,26},{... | collective-permute-start | bytes 24584 | tf_op jit(solution)/shard_map/ppermute | solution.py:12
  307.5 4.1 %fusion.3 = f32[3,16,64,128]{3,2,1,0:T(8,128)} fusion(f32[3,16,64,128]{3,2,1,0:T(8,128)S(1)} %copy-done.6, f32[1,16,64,128]{3,2,1,0:T(8,128)S(1)} %copy-done.10, f32[1,16,64,128]{3,2,1,0:T(8,128)S(1)} %copy-done.11, f32[1,16,64,128]{3,2,1,0:T(8,128)S(1)} %fusion.31, f32[1,16,64,128]{3,2,1,0:T(8,128)S(1)} %get-tuple-element.31, ...), kind=kLoop, calls=%fused_computation.7 | loop fusion | flops 3932160 | bytes 7864320 | tf_op jit(solution)/shard_map/add | solution.py:88
  (134 shorter events, 103.8 us)
Async XLA Ops:
  2.1 6.6 %collective-permute-start = (f32[6,16,1,128]{3,2,1,0:T(1,128)S(1)}, f32[6,16,1,128]{3,2,1,0:T(1,128)S(1)}, u32[]{:S(2)}, u32[]{:S(2)}) collective-permute-start(f32[6,16,1,128]{3,2,1,0:T(1,128)S(1)} %get-tuple-element.24), channel_id=1, source_target_pairs={{0,8},{8,16},{16,24},{1,9},{9,17},{17,25},{2,10},{10,18},{18,26},{... | collective-permute-start | bytes 147464 | tf_op jit(solution)/shard_map/ppermute | solution.py:12
  7.0 6.0 %collective-permute-start.1 = (f32[6,16,1,128]{3,2,1,0:T(1,128)S(1)}, f32[6,16,1,128]{3,2,1,0:T(1,128)S(1)}, u32[]{:S(2)}, u32[]{:S(2)}) collective-permute-start(f32[6,16,1,128]{3,2,1,0:T(1,128)S(1)} %get-tuple-element.25), channel_id=1, source_target_pairs={{8,0},{16,8},{24,16},{9,1},{17,9},{25,17},{10,2},{18,10},{26,18},{... | collective-permute-start | bytes 147464 | tf_op jit(solution)/shard_map/ppermute | solution.py:15
  20.2 7.5 %collective-permute-start.2 = (f32[6,16,66,1]{2,1,3,0:T(8,128)S(1)}, f32[6,16,66,1]{2,1,3,0:T(8,128)S(1)}, u32[]{:S(2)}, u32[]{:S(2)}) collective-permute-start(f32[6,16,66,1]{2,1,3,0:T(8,128)S(1)} %copy.5), channel_id=1, source_target_pairs={{0,2},{2,4},{4,6},{1,3},{3,5},{5,7},{8,10},{10,12},{12,14},{9,11},... | collective-permute-start | bytes 76040 | tf_op jit(solution)/shard_map/ppermute | solution.py:12
  26.5 6.0 %collective-permute-start.3 = (f32[6,16,66,1]{2,1,3,0:T(8,128)S(1)}, f32[6,16,66,1]{2,1,3,0:T(8,128)S(1)}, u32[]{:S(2)}, u32[]{:S(2)}) collective-permute-start(f32[6,16,66,1]{2,1,3,0:T(8,128)S(1)} %copy.6), channel_id=1, source_target_pairs={{2,0},{4,2},{6,4},{3,1},{5,3},{7,5},{10,8},{12,10},{14,12},{11,9},... | collective-permute-start | bytes 76040 | tf_op jit(solution)/shard_map/ppermute | solution.py:15
  48.8 5.7 %collective-permute-start.6 = (f32[16,1,128]{2,1,0:T(1,128)S(1)}, f32[16,1,128]{2,1,0:T(1,128)S(1)}, u32[]{:S(2)}, u32[]{:S(2)}) collective-permute-start(f32[16,1,128]{2,1,0:T(1,128)S(1)} %get-tuple-element.43), channel_id=1, source_target_pairs={{0,8},{8,16},{16,24},{1,9},{9,17},{17,25},{2,10},{10,18},{18,26},{... | collective-permute-start | bytes 24584 | tf_op jit(solution)/shard_map/ppermute | solution.py:12
  53.1 5.5 %collective-permute-start.7 = (f32[16,1,128]{2,1,0:T(1,128)S(1)}, f32[16,1,128]{2,1,0:T(1,128)S(1)}, u32[]{:S(2)}, u32[]{:S(2)}) collective-permute-start(f32[16,1,128]{2,1,0:T(1,128)S(1)} %get-tuple-element.44), channel_id=1, source_target_pairs={{8,0},{16,8},{24,16},{9,1},{17,9},{25,17},{10,2},{18,10},{26,18},{... | collective-permute-start | bytes 24584 | tf_op jit(solution)/shard_map/ppermute | solution.py:15
  59.2 5.0 %collective-permute-start.8 = (f32[16,66,1]{1,0,2:T(8,128)S(1)}, f32[16,66,1]{1,0,2:T(8,128)S(1)}, u32[]{:S(2)}, u32[]{:S(2)}) collective-permute-start(f32[16,66,1]{1,0,2:T(8,128)S(1)} %copy.9), channel_id=1, source_target_pairs={{0,2},{2,4},{4,6},{1,3},{3,5},{5,7},{8,10},{10,12},{12,14},{9,11},... | collective-permute-start | bytes 12680 | tf_op jit(solution)/shard_map/ppermute | solution.py:12
  62.9 5.6 %collective-permute-start.9 = (f32[16,66,1]{1,0,2:T(8,128)S(1)}, f32[16,66,1]{1,0,2:T(8,128)S(1)}, u32[]{:S(2)}, u32[]{:S(2)}) collective-permute-start(f32[16,66,1]{1,0,2:T(8,128)S(1)} %copy.10), channel_id=1, source_target_pairs={{2,0},{4,2},{6,4},{3,1},{5,3},{7,5},{10,8},{12,10},{14,12},{11,9},... | collective-permute-start | bytes 12680 | tf_op jit(solution)/shard_map/ppermute | solution.py:15
  122.2 4.7 %collective-permute-start.12 = (f32[8,1,64]{2,1,0:T(1,128)S(1)}, f32[8,1,64]{2,1,0:T(1,128)S(1)}, u32[]{:S(2)}, u32[]{:S(2)}) collective-permute-start(f32[8,1,64]{2,1,0:T(1,128)S(1)} %get-tuple-element.55), channel_id=1, source_target_pairs={{0,8},{8,16},{16,24},{1,9},{9,17},{17,25},{2,10},{10,18},{18,26},{... | collective-permute-start | bytes 6152 | tf_op jit(solution)/shard_map/ppermute | solution.py:12
  125.6 5.5 %collective-permute-start.13 = (f32[8,1,64]{2,1,0:T(1,128)S(1)}, f32[8,1,64]{2,1,0:T(1,128)S(1)}, u32[]{:S(2)}, u32[]{:S(2)}) collective-permute-start(f32[8,1,64]{2,1,0:T(1,128)S(1)} %get-tuple-element.56), channel_id=1, source_target_pairs={{8,0},{16,8},{24,16},{9,1},{17,9},{25,17},{10,2},{18,10},{26,18},{... | collective-permute-start | bytes 6152 | tf_op jit(solution)/shard_map/ppermute | solution.py:15
  131.2 6.3 %collective-permute-start.14 = (f32[8,34,1]{2,1,0:T(8,128)S(1)}, f32[8,34,1]{2,1,0:T(8,128)S(1)}, u32[]{:S(2)}, u32[]{:S(2)}) collective-permute-start(f32[8,34,1]{2,1,0:T(8,128)S(1)} %get-tuple-element.52), channel_id=1, source_target_pairs={{0,2},{2,4},{4,6},{1,3},{3,5},{5,7},{8,10},{10,12},{12,14},{9,11},... | collective-permute-start | bytes 3272 | tf_op jit(solution)/shard_map/ppermute | solution.py:12
  134.7 7.2 %collective-permute-start.15 = (f32[8,34,1]{2,1,0:T(8,128)S(1)}, f32[8,34,1]{2,1,0:T(8,128)S(1)}, u32[]{:S(2)}, u32[]{:S(2)}) collective-permute-start(f32[8,34,1]{2,1,0:T(8,128)S(1)} %get-tuple-element.51), channel_id=1, source_target_pairs={{2,0},{4,2},{6,4},{3,1},{5,3},{7,5},{10,8},{12,10},{14,12},{11,9},... | collective-permute-start | bytes 3272 | tf_op jit(solution)/shard_map/ppermute | solution.py:15
  151.0 5.5 %collective-permute-start.19 = (f32[8,1,64]{2,1,0:T(1,128)S(1)}, f32[8,1,64]{2,1,0:T(1,128)S(1)}, u32[]{:S(2)}, u32[]{:S(2)}) collective-permute-start(f32[8,1,64]{2,1,0:T(1,128)S(1)} %get-tuple-element.54), channel_id=1, source_target_pairs={{8,0},{16,8},{24,16},{9,1},{17,9},{25,17},{10,2},{18,10},{26,18},{... | collective-permute-start | bytes 6152 | tf_op jit(solution)/shard_map/ppermute | solution.py:15
  156.6 5.4 %collective-permute-start.20 = (f32[8,34,1]{2,1,0:T(8,128)S(1)}, f32[8,34,1]{2,1,0:T(8,128)S(1)}, u32[]{:S(2)}, u32[]{:S(2)}) collective-permute-start(f32[8,34,1]{2,1,0:T(8,128)S(1)} %get-tuple-element.50), channel_id=1, source_target_pairs={{0,2},{2,4},{4,6},{1,3},{3,5},{5,7},{8,10},{10,12},{12,14},{9,11},... | collective-permute-start | bytes 3272 | tf_op jit(solution)/shard_map/ppermute | solution.py:12
  159.3 7.2 %collective-permute-start.21 = (f32[8,34,1]{2,1,0:T(8,128)S(1)}, f32[8,34,1]{2,1,0:T(8,128)S(1)}, u32[]{:S(2)}, u32[]{:S(2)}) collective-permute-start(f32[8,34,1]{2,1,0:T(8,128)S(1)} %get-tuple-element.49), channel_id=1, source_target_pairs={{2,0},{4,2},{6,4},{3,1},{5,3},{7,5},{10,8},{12,10},{14,12},{11,9},... | collective-permute-start | bytes 3272 | tf_op jit(solution)/shard_map/ppermute | solution.py:15
  253.4 5.5 %collective-permute-start.24 = (f32[16,1,128]{2,1,0:T(1,128)S(1)}, f32[16,1,128]{2,1,0:T(1,128)S(1)}, u32[]{:S(2)}, u32[]{:S(2)}) collective-permute-start(f32[16,1,128]{2,1,0:T(1,128)S(1)} %get-tuple-element.41), channel_id=1, source_target_pairs={{0,8},{8,16},{16,24},{1,9},{9,17},{17,25},{2,10},{10,18},{18,26},{... | collective-permute-start | bytes 24584 | tf_op jit(solution)/shard_map/ppermute | solution.py:12
  257.5 5.5 %collective-permute-start.25 = (f32[16,1,128]{2,1,0:T(1,128)S(1)}, f32[16,1,128]{2,1,0:T(1,128)S(1)}, u32[]{:S(2)}, u32[]{:S(2)}) collective-permute-start(f32[16,1,128]{2,1,0:T(1,128)S(1)} %get-tuple-element.42), channel_id=1, source_target_pairs={{8,0},{16,8},{24,16},{9,1},{17,9},{25,17},{10,2},{18,10},{26,18},{... | collective-permute-start | bytes 24584 | tf_op jit(solution)/shard_map/ppermute | solution.py:15
  263.6 5.5 %collective-permute-start.26 = (f32[16,66,1]{1,0,2:T(8,128)S(1)}, f32[16,66,1]{1,0,2:T(8,128)S(1)}, u32[]{:S(2)}, u32[]{:S(2)}) collective-permute-start(f32[16,66,1]{1,0,2:T(8,128)S(1)} %copy.15), channel_id=1, source_target_pairs={{0,2},{2,4},{4,6},{1,3},{3,5},{5,7},{8,10},{10,12},{12,14},{9,11},... | collective-permute-start | bytes 12680 | tf_op jit(solution)/shard_map/ppermute | solution.py:12
  267.8 5.6 %collective-permute-start.27 = (f32[16,66,1]{1,0,2:T(8,128)S(1)}, f32[16,66,1]{1,0,2:T(8,128)S(1)}, u32[]{:S(2)}, u32[]{:S(2)}) collective-permute-start(f32[16,66,1]{1,0,2:T(8,128)S(1)} %copy.16), channel_id=1, source_target_pairs={{2,0},{4,2},{6,4},{3,1},{5,3},{7,5},{10,8},{12,10},{14,12},{11,9},... | collective-permute-start | bytes 12680 | tf_op jit(solution)/shard_map/ppermute | solution.py:15
  273.9 4.6 %collective-permute-start.28 = (f32[1,66,130]{2,1,0:T(8,128)S(1)}, f32[1,66,130]{2,1,0:T(8,128)S(1)}, u32[]{:S(2)}, u32[]{:S(2)}) collective-permute-start(f32[1,66,130]{2,1,0:T(8,128)S(1)} %get-tuple-element.26), channel_id=1, source_target_pairs={{1,0},{3,2},{5,4},{7,6},{9,8},{11,10},{13,12},{15,14},{17,16},{19,... | collective-permute-start | bytes 102968 | tf_op jit(solution)/shard_map/ppermute | solution.py:15
  281.2 7.2 %collective-permute-start.30 = (f32[16,1,128]{2,1,0:T(1,128)S(1)}, f32[16,1,128]{2,1,0:T(1,128)S(1)}, u32[]{:S(2)}, u32[]{:S(2)}) collective-permute-start(f32[16,1,128]{2,1,0:T(1,128)S(1)} %get-tuple-element.39), channel_id=1, source_target_pairs={{0,8},{8,16},{16,24},{1,9},{9,17},{17,25},{2,10},{10,18},{18,26},{... | collective-permute-start | bytes 24584 | tf_op jit(solution)/shard_map/ppermute | solution.py:12
  285.7 5.5 %collective-permute-start.31 = (f32[16,1,128]{2,1,0:T(1,128)S(1)}, f32[16,1,128]{2,1,0:T(1,128)S(1)}, u32[]{:S(2)}, u32[]{:S(2)}) collective-permute-start(f32[16,1,128]{2,1,0:T(1,128)S(1)} %get-tuple-element.40), channel_id=1, source_target_pairs={{8,0},{16,8},{24,16},{9,1},{17,9},{25,17},{10,2},{18,10},{26,18},{... | collective-permute-start | bytes 24584 | tf_op jit(solution)/shard_map/ppermute | solution.py:15
  293.8 7.6 %collective-permute-start.32 = (f32[16,66,1]{1,0,2:T(8,128)S(1)}, f32[16,66,1]{1,0,2:T(8,128)S(1)}, u32[]{:S(2)}, u32[]{:S(2)}) collective-permute-start(f32[16,66,1]{1,0,2:T(8,128)S(1)} %copy.21), channel_id=1, source_target_pairs={{0,2},{2,4},{4,6},{1,3},{3,5},{5,7},{8,10},{10,12},{12,14},{9,11},... | collective-permute-start | bytes 12680 | tf_op jit(solution)/shard_map/ppermute | solution.py:12
  297.7 5.6 %collective-permute-start.33 = (f32[16,66,1]{1,0,2:T(8,128)S(1)}, f32[16,66,1]{1,0,2:T(8,128)S(1)}, u32[]{:S(2)}, u32[]{:S(2)}) collective-permute-start(f32[16,66,1]{1,0,2:T(8,128)S(1)} %copy.22), channel_id=1, source_target_pairs={{2,0},{4,2},{6,4},{3,1},{5,3},{7,5},{10,8},{12,10},{14,12},{11,9},... | collective-permute-start | bytes 12680 | tf_op jit(solution)/shard_map/ppermute | solution.py:15
  (24 other events, 152.8 us)
where the time goes:
time: 313 us; the launch traced here: 312 us
  local copies, waits for them, and re-layouts  96.2 us (31%)
  starting transfers between devices  80.9 us (26%)
  waiting for transfers between devices  54.6 us (17%)
  blocking collectives  38 us (12%)
  other arithmetic  34.1 us (11%)
  between operations  7.79 us (2%)
    ppermute x17, starting transfers between devices, with_halo(): lax.ppermute(lax.slice_in_dim(block, block.shape[dim] - width, None, axis...  57.2 us
    ppermute x18, waiting for transfers between devices, with_halo(): lax.ppermute(lax.slice_in_dim(block, 0, width, axis=dim), axis, backward)  47.6 us
    psum x1, blocking collectives, local(): lax.psum((jnp.sum(first_dir * coarse_rhs), jnp.sum(second_dir * coarse_rh...  38 us
    reshape x1, local copies, waits for them, and re-layouts, local(): node_res.reshape(sx // 2, 2, sy // 2, 2, sz // 2, 2).sum(axis=(1, 3, 5))  34.9 us
    reshape x1, local copies, waits for them, and re-layouts, local(): spread = jnp.broadcast_to(coarse_sol[:, None, :, None, :, None], (sx // 2...  24 us
    ppermute x18, starting transfers between devices, with_halo(): lax.ppermute(lax.slice_in_dim(block, 0, width, axis=dim), axis, backward)  23.7 us
    reduce_sum x1, other arithmetic, local(): node_res.reshape(sx // 2, 2, sy // 2, 2, sz // 2, 2).sum(axis=(1, 3, 5))  12.2 us
    broadcast_in_dim x1, local copies, waits for them, and re-layouts, local(): jnp.broadcast_to(coarse_sol[:, None, :, None, :, None], (sx // 2, 2, sy /...  11.4 us
  transfers between devices with their start and end apart: 35, of which 22 were waited for; matrix products, arithmetic and copies ran while one was open for 4% of the time, Pallas kernels for 0%

commit v1 on v0

v1 whole, which is shorter than its diff:
```python
import functools

import jax
import jax.numpy as jnp
from jax import lax
from jax.experimental import pallas as pl
from jax.experimental.pallas import tpu as pltpu
from jax.sharding import PartitionSpec as P

MESH = pl.DeviceIdType.MESH
AXES = ("gz", "gx", "gy")
FGI, V1I, V2I, F0I = 3, 4, 5, 6
PAD = 8


def kernel(
    sizes,
    res, dia, shf, csh, out,
    R, D, NI, CS, S, FG, CI, CR, A1, T, V1, V2, F, FN, OB,
    SX, RX, SY, RY, PZ, PX, PY,
    in_sem, out_sem, send_sem, recv_sem, psend, precv,
):
    n0, n1, n2 = NI.shape
    m0, m1, m2 = CS.shape
    groups = n1 // 8
    me = [lax.axis_index(a) for a in AXES]
    rows = pl.ds(PAD, n1)

    loads = []
    for k in (2, 1, 0):
        for src, dst in ((res, R), (dia, D)):
            loads.append(pltpu.make_async_copy(src.at[k], dst.at[k], in_sem.at[len(loads)]))
    loads.append(pltpu.make_async_copy(shf, NI, in_sem.at[6]))
    loads.append(pltpu.make_async_copy(csh, CS, in_sem.at[7]))
    for c in loads:
        c.start()

    zplane = jnp.zeros((n1, n2), jnp.float32)
    for k in range(3):
        S[k, 0, rows] = zplane
        S[k, n0 + 1, rows] = zplane
        F[k, n0] = zplane
    FG[0, rows] = zplane
    FG[n0 + 1, rows] = zplane
    for V in (V1, V2):
        V[0, rows] = zplane
        V[m0 + 1, rows] = zplane
    RX[...] = jnp.zeros(RX.shape, jnp.float32)
    RY[...] = jnp.zeros(RY.shape, jnp.float32)
    barrier = pltpu.get_barrier_semaphore()
    total = 0
    for a in range(3):
        for d in range(1, sizes[a]):
            pl.semaphore_signal(
                barrier, inc=1, device_id={AXES[a]: lax.rem(me[a] + d, sizes[a])}, device_id_type=MESH
            )
            total += 1

    lane = lax.broadcasted_iota(jnp.int32, (8, n2), 1)
    lane_full = lax.broadcasted_iota(jnp.int32, (n1, n2), 1)
    row_full = lax.broadcasted_iota(jnp.int32, (n1, n2), 0)
    keys = {p: ((lane + p // 2) // p) % (n2 // p) for p in (2, 4)}
    is_low = {p: (lane % p) >= p // 2 for p in (2, 4)}

    def place(i, g, p):
        k = i * groups + g
        per = n2 // p
        return k // per, k % per

    def pack(f, plane, count, p):
        accs = [jnp.zeros((8, n2), jnp.float32) for _ in range(place(count - 1, groups - 1, p)[0] + 1)]
        for i in range(count):
            x = plane(i)
            for g in range(groups):
                v, kk = place(i, g, p)
                part = x[8 * g : 8 * g + 8]
                if kk:
                    part = pltpu.roll(part, p * kk, 1)
                accs[v] = jnp.where(keys[p] == kk, part, accs[v])
        for v, acc in enumerate(accs):
            SY[f, v] = acc

    def arrived(f, p):
        return [jnp.where(is_low[p], RY[f, 0, v], RY[f, 1, v]) for v in range(RY.shape[2])]

    def halo(ws, i, p):
        parts = []
        for g in range(groups):
            v, kk = place(i, g, p)
            parts.append(pltpu.roll(ws[v], n2 - p * kk, 1) if kk else ws[v])
        return jnp.concatenate(parts, axis=0)

    def from_low(x, h, sh=1):
        return pltpu.roll(jnp.where(lane_full >= n2 - sh, h, x), sh, 1)

    def from_high(x, h, sh=1):
        return pltpu.roll(jnp.where(lane_full < sh, h, x), n2 - sh, 1)

    def inplane(ref, x, h, sh):
        near = ref[pl.ds(PAD - sh, n1)] + ref[pl.ds(PAD + sh, n1)]
        return near + from_low(x, h, sh) + from_high(x, h, sh)

    def field(f):
        if f < 3:
            return S.at[f], n0
        return {FGI: (FG, n0), V1I: (V1, m0), V2I: (V2, m0)}[f]

    def message(f, a, d):
        if a == 0:
            if f >= F0I:
                src, dst = F.at[f - F0I, 0], F.at[f - F0I, n0]
            else:
                ref, n = field(f)
                src = ref.at[n if d else 1, rows]
                dst = ref.at[0 if d else n + 1, rows]
        elif a == 1:
            count = m0 if f in (V1I, V2I) else n0
            src, dst = SX.at[f, d, pl.ds(0, count)], RX.at[f, 1 - d, pl.ds(0, count)]
        else:
            src, dst = SY.at[f], RY.at[f, 1 - d]
        step = 1 if d else -1
        return pltpu.make_async_remote_copy(
            src_ref=src, dst_ref=dst, send_sem=send_sem.at[f, a, d], recv_sem=recv_sem.at[f, a, d],
            device_id={AXES[a]: lax.rem(me[a] + step + sizes[a], sizes[a])}, device_id_type=MESH,
        )

    def dirs(f):
        return (0,) if f >= F0I else (0, 1)

    def can_send(a, d):
        return me[a] < sizes[a] - 1 if d else me[a] > 0

    def send(f, a):
        for d in dirs(f):
            pl.when(can_send(a, d))(lambda f=f, a=a, d=d: message(f, a, d).start())

    def receive(f, a):
        for d in dirs(f):
            pl.when(can_send(a, 1 - d))(lambda f=f, a=a, d=d: message(f, a, d).wait_recv())

    def faces_x(f, get, count):
        for i in range(count):
            SX[f, 0, i : i + 1] = get(i, 0)
            if f < F0I:
                SX[f, 1, i : i + 1] = get(i, n1 - 1)

    def rows_x(f, width):
        ref, count = field(f)
        for i in range(count):
            for w in range(width):
                ref[1 + i, PAD - 1 - w : PAD - w] = RX[f, 0, i : i + 1]
                ref[1 + i, PAD + n1 + w : PAD + n1 + w + 1] = RX[f, 1, i : i + 1]

    def exchange(f, p):
        ref, count = field(f)
        send(f, 0)
        faces_x(f, lambda i, r: ref[1 + i, PAD + r : PAD + r + 1], count)
        send(f, 1)
        pack(f, lambda i: ref[1 + i, rows], count, p)
        send(f, 2)

    for pos, k in enumerate((2, 1, 0)):
        loads[2 * pos].wait()
        loads[2 * pos + 1].wait()
        for i in range(n0):
            inv = 1.0 / D[k, i]
            D[k, i] = inv
            S[k, 1 + i, rows] = R[k, i] * inv

    pl.semaphore_wait(barrier, total)

    def one(f, a):
        ref, count = field(f)
        if a == 1:
            faces_x(f, lambda i, r: ref[1 + i, PAD + r : PAD + r + 1], count)
        if a == 2:
            pack(f, lambda i: ref[1 + i, rows], count, 2)
        send(f, a)

    one(1, 1)
    one(2, 2)
    one(0, 0)
    for f, a in ((0, 1), (2, 1), (1, 0), (2, 0), (0, 2), (1, 2)):
        one(f, a)

    loads[6].wait()
    for i in range(n0):
        NI[i] = 1.0 / (6.0 + NI[i])
    loads[7].wait()
    spread_rows = (
        lax.broadcasted_iota(jnp.int32, (n1, m1), 0) // 2 == lax.broadcasted_iota(jnp.int32, (n1, m1), 1)
    ).astype(jnp.float32)
    spread_cols = (
        lax.broadcasted_iota(jnp.int32, (m2, n2), 1) // 2 == lax.broadcasted_iota(jnp.int32, (m2, n2), 0)
    ).astype(jnp.float32)
    exact = functools.partial(
        jnp.dot, precision=lax.Precision.HIGHEST, preferred_element_type=jnp.float32
    )
    for i in range(m0):
        CI[i] = exact(spread_rows, exact(1.0 / (6.0 + CS[i]), spread_cols))

    receive(1, 1)
    rows_x(1, 1)
    receive(0, 0)
    receive(2, 2)
    ws = arrived(2, 2)
    for i in range(n0):
        x2 = S[2, 1 + i, rows]
        rhs = S[0, i, rows] - S[0, 1 + i, rows]
        rhs = rhs + (S[1, 1 + i, pl.ds(PAD - 1, n1)] - S[1, 1 + i, rows])
        rhs = rhs + (from_low(x2, halo(ws, i, 2)) - x2)
        FG[1 + i, rows] = rhs * NI[i]
    exchange(FGI, 2)

    def smooth(k):
        for a in range(3):
            if (k, a) not in ((1, 1), (0, 0), (2, 2)):
                receive(k, a)
        if k != 1:
            rows_x(k, 1)
        w = arrived(k, 2)
        for i in range(n0):
            x = S[k, 1 + i, rows]
            near = S[k, i, rows] + S[k, i + 2, rows] + inplane(S.at[k, 1 + i], x, halo(w, i, 2), 1)
            OB[k, i] = x + near * D[k, i]

    smooth(0)

    for a in range(3):
        receive(FGI, a)
    rows_x(FGI, 1)
    ws = arrived(FGI, 2)
    for c in range(m0):
        t = None
        for i in (2 * c, 2 * c + 1):
            x = FG[1 + i, rows]
            near = FG[i, rows] + FG[i + 2, rows] + inplane(FG.at[1 + i], x, halo(ws, i, 2), 1)
            F[0, i] = near
            t = near if t is None else t + near
        t = t + jnp.where(lane_full % 2 == 0, pltpu.roll(t, n2 - 1, 1), pltpu.roll(t, 1, 1))
        T[c, rows] = t
        t = t + jnp.where(row_full % 2 == 0, T[c, pl.ds(PAD + 1, n1)], T[c, pl.ds(PAD - 1, n1)])
        CR[c] = t
        V1[1 + c, rows] = t * CI[c]
    exchange(V1I, 4)

    def faces_f(j):
        f = F0I + j
        send(f, 0)
        faces_x(f, lambda i, r: F[j, i, r : r + 1], n0)
        send(f, 1)
        pack(f, lambda i: F[j, i], n0, 2)
        send(f, 2)

    for i in range(n0):
        F[0, i] = FG[1 + i, rows] + F[0, i] * NI[i]
    faces_f(0)
    smooth(1)

    for a in range(3):
        receive(V1I, a)
    rows_x(V1I, 2)
    ws1 = arrived(V1I, 4)
    for c in range(m0):
        x = V1[1 + c, rows]
        near = V1[c, rows] + V1[c + 2, rows] + inplane(V1.at[1 + c], x, halo(ws1, c, 4), 2)
        A1[c] = CR[c] - near
        V2[1 + c, rows] = x - near * CI[c]
    exchange(V2I, 4)

    def fold(x):
        acc = x[0:8]
        for g in range(1, groups):
            acc = acc + x[8 * g : 8 * g + 8]
        return acc

    def spread_near(j, V, w):
        for c in range(m0):
            x = V[1 + c, rows]
            near = x + inplane(V.at[1 + c], x, halo(w, c, 4), 1)
            F[j, 2 * c] = (near + V[c, rows]) * NI[2 * c]
            F[j, 2 * c + 1] = (near + V[c + 2, rows]) * NI[2 * c + 1]
        faces_f(j)

    sums = [jnp.zeros((8, n2), jnp.float32) for _ in range(5)]
    for c in range(m0):
        v1, v2, a1, cr = V1[1 + c, rows], V2[1 + c, rows], A1[c], CR[c]
        sums[0] = sums[0] + fold(v1 * cr)
        sums[1] = sums[1] + fold(v2 * cr)
        sums[2] = sums[2] + fold(v1 * a1)
        sums[3] = sums[3] + fold(v2 * a1)
    spread_near(1, V1, ws1)

    for a in range(3):
        receive(V2I, a)
    rows_x(V2I, 2)
    ws2 = arrived(V2I, 4)
    for c in range(m0):
        x = V2[1 + c, rows]
        near = V2[c, rows] + V2[c + 2, rows] + inplane(V2.at[1 + c], x, halo(ws2, c, 4), 2)
        sums[4] = sums[4] + fold(x * (A1[c] - near))
    part = jnp.concatenate(
        [jnp.sum(s, axis=0, keepdims=True) for s in sums] + [jnp.zeros((3, n2), jnp.float32)], axis=0
    )

    bases = (0, sizes[0], sizes[0] + sizes[1])

    def sum_message(a, slots, d):
        return pltpu.make_async_remote_copy(
            src_ref=slots.at[me[a]], dst_ref=slots.at[me[a]],
            send_sem=psend.at[bases[a] + d], recv_sem=precv.at[bases[a] + d],
            device_id={AXES[a]: lax.rem(me[a] + d, sizes[a])}, device_id_type=MESH,
        )

    def sum_start(a, slots, value):
        slots[me[a]] = value
        for d in range(1, sizes[a]):
            sum_message(a, slots, d).start()

    def sum_end(a, slots):
        for d in range(1, sizes[a]):
            src = lax.rem(me[a] + sizes[a] - d, sizes[a])
            pltpu.make_async_remote_copy(
                src_ref=slots.at[src], dst_ref=slots.at[src],
                send_sem=psend.at[bases[a] + d], recv_sem=precv.at[bases[a] + d],
                device_id={AXES[a]: src}, device_id_type=MESH,
            ).wait_recv()
        value = slots[0]
        for d in range(1, sizes[a]):
            value = value + slots[d]
        return value

    sum_start(0, PZ, part)
    part = sum_end(0, PZ)
    sum_start(1, PX, part)
    spread_near(2, V2, ws2)
    part = sum_end(1, PX)
    sum_start(2, PY, part)
    smooth(2)
    for j in range(3):
        for a in range(3):
            receive(F0I + j, a)
    part = sum_end(2, PY)
    tot = jnp.sum(part, axis=1, keepdims=True)
    gone, gtwo, hone, hmix, htwo = [tot[q : q + 1] for q in range(5)]
    two = (gtwo - hmix * gone / hone) / (htwo - hmix * hmix / hone)
    oneco = (gone - hmix * two) / hone

    def mix(get):
        a = get(0)
        return a + jnp.broadcast_to(oneco, a.shape) * get(1) + jnp.broadcast_to(two, a.shape) * get(2)

    for i in range(n0 + 1):
        FN[i, 0:n1] = mix(lambda j: F[j, i])
    for i in range(n0):
        FN[i, n1 : n1 + 1] = mix(lambda j: RX[F0I + j, 1, i : i + 1])
    wf = [mix(lambda j: RY[F0I + j, 1, v]) for v in range(RY.shape[2])]
    stores = []
    for i in range(n0):
        x = FN[i, 0:n1]
        OB[0, i] = OB[0, i] + (FN[i + 1, 0:n1] - x)
        OB[1, i] = OB[1, i] + (FN[i, 1 : n1 + 1] - x)
        OB[2, i] = OB[2, i] + (from_high(x, halo(wf, i, 2)) - x)
        if i % 4 == 3 or i == n0 - 1:
            lo = 4 * (i // 4)
            for k in range(3):
                part_of = pl.ds(lo, i + 1 - lo)
                copy = pltpu.make_async_copy(OB.at[k, part_of], out.at[k, part_of], out_sem.at[len(stores)])
                copy.start()
                stores.append(copy)

    for a, slots in ((0, PZ), (1, PX), (2, PY)):
        for d in range(1, sizes[a]):
            sum_message(a, slots, d).wait_send()
    for a in range(3):
        for d in (0, 1):
            def drain(a=a, d=d):
                for f in range(9):
                    if d in dirs(f):
                        message(f, a, d).wait_send()
            pl.when(can_send(a, d))(drain)
    for copy in stores:
        copy.wait()


def solution(mesh):
    sizes = tuple(mesh.shape[a] for a in AXES)

    def local(residual, edge_diag, node_shift, coarse_shift):
        n0, n1, n2 = node_shift.shape
        m0, m1, m2 = coarse_shift.shape
        vecs = max(-(-(n0 * (n1 // 8)) // (n2 // 2)), -(-(m0 * (n1 // 8)) // (n2 // 4)))
        f32 = jnp.float32
        V = lambda *s: pltpu.VMEM(s, f32)
        scratch = [
            V(3, n0, n1, n2), V(3, n0, n1, n2), V(n0, n1, n2), V(m0, m1, m2),
            V(3, n0 + 2, n1 + 2 * PAD, n2), V(n0 + 2, n1 + 2 * PAD, n2),
            V(m0, n1, n2), V(m0, n1, n2), V(m0, n1, n2), V(m0, n1 + 2 * PAD, n2),
            V(m0 + 2, n1 + 2 * PAD, n2), V(m0 + 2, n1 + 2 * PAD, n2),
            V(3, n0 + 1, n1, n2), V(n0 + 1, n1 + PAD, n2), V(3, n0, n1, n2),
            V(9, 2, n0, n2), V(9, 2, n0, n2), V(9, vecs, 8, n2), V(9, 2, vecs, 8, n2),
            V(sizes[0], 8, n2), V(sizes[1], 8, n2), V(sizes[2], 8, n2),
            pltpu.SemaphoreType.DMA((8,)), pltpu.SemaphoreType.DMA((3 * (-(-n0 // 4)),)),
            pltpu.SemaphoreType.DMA((9, 3, 2)), pltpu.SemaphoreType.DMA((9, 3, 2)),
            pltpu.SemaphoreType.DMA((sum(sizes),)), pltpu.SemaphoreType.DMA((sum(sizes),)),
        ]
        return pl.pallas_call(
            functools.partial(kernel, sizes),
            out_shape=jax.ShapeDtypeStruct(residual.shape, f32),
            in_specs=[pl.BlockSpec(memory_space=pl.ANY)] * 4,
            out_specs=pl.BlockSpec(memory_space=pl.ANY),
            scratch_shapes=scratch,
            compiler_params=pltpu.CompilerParams(collective_id=0, has_side_effects=True),
        )(residual, edge_diag, node_shift, coarse_shift)

    placed = (
        P(None, "gz", "gx", "gy"),
        P(None, "gz", "gx", "gy"),
        P("gz", "gx", "gy"),
        P("gz", "gx", "gy"),
    )
    return jax.shard_map(
        local, mesh=mesh, in_specs=placed, out_specs=P(None, "gz", "gx", "gy"), check_vma=False
    )
```

time: 313 us -> 33.7 us (0.11)
  local copies, waits for them, and re-layouts: 96.2 us -> 2.73 us
  starting transfers between devices: 80.9 us -> 0 us
  waiting for transfers between devices: 54.6 us -> 0 us
  blocking collectives: 38 us -> 0 us
  other arithmetic: 34.1 us -> 0 us
  Pallas kernels: 0 us -> 30.8 us
  between operations: 7.79 us -> 0.01 us
    ppermute x35 -> x0, starting transfers between devices: 80.9 us -> none  [the longest x17 57.2 us: with_halo(): lax.ppermute(lax.slice_in_dim(block, block.shape[dim] - width, None, axis...]
    reshape x2 -> x0, local copies, waits for them, and re-layouts: 58.9 us -> none  [the longest x1 34.9 us: local(): node_res.reshape(sx // 2, 2, sy // 2, 2, sz // 2, 2).sum(axis=(1, 3, 5))]
    ppermute x35 -> x0, waiting for transfers between devices: 54.6 us -> none  [the longest x18 47.6 us: with_halo(): lax.ppermute(lax.slice_in_dim(block, 0, width, axis=dim), axis, backward)]
    psum x1 -> x0, blocking collectives: 38 us -> none  [local(): lax.psum((jnp.sum(first_dir * coarse_rhs), jnp.sum(second_dir * coarse_rh...]
    pallas_call x0 -> x1, Pallas kernels: none -> 30.8 us  [local(): pl.pallas_call(functools.partial(kernel, sizes), out_shape=jax.ShapeDtype...]
    slice x20 -> x0, local copies, waits for them, and re-layouts: 14.9 us -> none  [the longest x12 9.78 us: with_halo(): lax.slice_in_dim(block, block.shape[dim] - width, None, axis=dim)]
    reduce_sum x3 -> x0, other arithmetic: 14.2 us -> none  [the longest x1 12.2 us: local(): node_res.reshape(sx // 2, 2, sy // 2, 2, sz // 2, 2).sum(axis=(1, 3, 5))]
    broadcast_in_dim x1 -> x0, local copies, waits for them, and re-layouts: 11.4 us -> none  [local(): jnp.broadcast_to(coarse_sol[:, None, :, None, :, None], (sx // 2, 2, sy /...]
  transfers between devices with their start and end apart: 35 -> 0, of which waited for: 22 -> 0; matrix products, arithmetic and copies ran while one was open for 4% -> 0% of each run, Pallas kernels for 0% -> 0%
where the time goes in v1:
time: 33.7 us; the launch traced here: 33.6 us
  Pallas kernels  30.8 us (91%)
  local copies, waits for them, and re-layouts  2.73 us (8%)
    pallas_call x1, Pallas kernels, local(): pl.pallas_call(functools.partial(kernel, sizes), out_shape=jax.ShapeDtype...  30.8 us
    unnamed x1, local copies, waits for them, and re-layouts  2.73 us

profile of v1, /device:TPU:0, one launch (start us, length us, event | category | flops | bytes accessed | tf_op | source)
XLA Modules:
  0.0 33.6 jit_solution(17943745395505647240)
XLA Ops:
  0.0 30.8 %shard_map.46 = f32[3,16,64,128]{3,2,1,0:T(8,128)} custom-call(f32[3,16,64,128]{3,2,1,0:T(8,128)} %res.1, f32[3,16,64,128]{3,2,1,0:T(8,128)} %dia.1, f32[16,64,128]{2,1,0:T(8,128)} %shf.1, f32[8,32,64]{2,1,0:T(8,128)} %csh.1), custom_call_target="tpu_custom_call" | custom-call | tf_op jit(solution)/shard_map/pallas_call | solution.py:407
  30.8 2.7 %copy.6 = f32[3,16,64,128]{3,2,1,0:T(8,128)} copy(f32[3,16,64,128]{3,2,1,0:T(8,128)} %shard_map.46) | data formatting | bytes 3145728

commit v2 on v1

--- a/solution.py
+++ b/solution.py
@@ -1,4 +1,6 @@
 import functools
+import itertools
+import math
 
 import jax
 import jax.numpy as jnp
@@ -11,14 +13,15 @@
 AXES = ("gz", "gx", "gy")
 FGI, V1I, V2I, F0I = 3, 4, 5, 6
 PAD = 8
+PHASES = ((0, 1), (2,))
 
 
 def kernel(
     sizes,
-    res, dia, shf, csh, out,
-    R, D, NI, CS, S, FG, CI, CR, A1, T, V1, V2, F, FN, OB,
-    SX, RX, SY, RY, PZ, PX, PY,
-    in_sem, out_sem, send_sem, recv_sem, psend, precv,
+    res, dia, shf, csh, OB,
+    R, D, NI, CS, S, FG, CI, CR, A1, T, V1, V2, F, FN,
+    SX, RX, SY, RY, PA, PB,
+    in_sem, send_sem, recv_sem, psend, precv,
 ):
     n0, n1, n2 = NI.shape
     m0, m1, m2 = CS.shape
@@ -26,8 +29,17 @@
     me = [lax.axis_index(a) for a in AXES]
     rows = pl.ds(PAD, n1)
 
+    def offsets(axes):
+        every = itertools.product(*[range(sizes[a]) for a in axes])
+        return [offs for offs in every if any(offs)]
+
+    def partner(axes, offs, sign):
+        return {
+            AXES[a]: lax.rem(me[a] + (o if sign > 0 else sizes[a] - o), sizes[a]) for a, o in zip(axes, offs)
+        }
+
     loads = []
-    for k in (2, 1, 0):
+    for k in (1, 2, 0):
         for src, dst in ((res, R), (dia, D)):
             loads.append(pltpu.make_async_copy(src.at[k], dst.at[k], in_sem.at[len(loads)]))
     loads.append(pltpu.make_async_copy(shf, NI, in_sem.at[6]))
@@ -49,16 +61,15 @@
     RY[...] = jnp.zeros(RY.shape, jnp.float32)
     barrier = pltpu.get_barrier_semaphore()
     total = 0
-    for a in range(3):
-        for d in range(1, sizes[a]):
-            pl.semaphore_signal(
-                barrier, inc=1, device_id={AXES[a]: lax.rem(me[a] + d, sizes[a])}, device_id_type=MESH
-            )
+    for axes in PHASES:
+        for offs in offsets(axes):
+            pl.semaphore_signal(barrier, inc=1, device_id=partner(axes, offs, 1), device_id_type=MESH)
             total += 1
 
     lane = lax.broadcasted_iota(jnp.int32, (8, n2), 1)
     lane_full = lax.broadcasted_iota(jnp.int32, (n1, n2), 1)
     row_full = lax.broadcasted_iota(jnp.int32, (n1, n2), 0)
+    row8 = lax.broadcasted_iota(jnp.int32, (8, n2), 0)
     keys = {p: ((lane + p // 2) // p) % (n2 // p) for p in (2, 4)}
     is_low = {p: (lane % p) >= p // 2 for p in (2, 4)}
 
@@ -99,6 +110,37 @@
     def inplane(ref, x, h, sh):
         near = ref[pl.ds(PAD - sh, n1)] + ref[pl.ds(PAD + sh, n1)]
         return near + from_low(x, h, sh) + from_high(x, h, sh)
+
+    def local_near(ref, i, n, sh):
+        x = ref[1 + i, rows]
+        near = jnp.where(row_full >= sh, ref[1 + i, pl.ds(PAD - sh, n1)], 0.0)
+        near = near + jnp.where(row_full < n1 - sh, ref[1 + i, pl.ds(PAD + sh, n1)], 0.0)
+        near = near + jnp.where(lane_full >= sh, pltpu.roll(x, sh, 1), 0.0)
+        near = near + jnp.where(lane_full < n2 - sh, pltpu.roll(x, n2 - sh, 1), 0.0)
+        if i > 0:
+            near = near + ref[i, rows]
+        if i < n - 1:
+            near = near + ref[i + 2, rows]
+        return near
+
+    def edges(f, p):
+        sh = p // 2
+        return [
+            jnp.where(is_low[p], pltpu.roll(RY[f, 1, v], n2 - sh, 1), pltpu.roll(RY[f, 0, v], sh, 1))
+            for v in range(RY.shape[2])
+        ]
+
+    def outer_near(near, ref, f, ws, i, n, p):
+        sh = p // 2
+        if i == 0:
+            near = near + ref[0, rows]
+        if i == n - 1:
+            near = near + ref[n + 1, rows]
+        side = (lane_full < sh) | (lane_full >= n2 - sh)
+        near = near + jnp.where(side, halo(ws, i, p), 0.0)
+        low = near[0:8] + jnp.where(row8 < sh, RX[f, 0, i : i + 1], 0.0)
+        high = near[n1 - 8 : n1] + jnp.where(row8 >= 8 - sh, RX[f, 1, i : i + 1], 0.0)
+        return jnp.concatenate([low, near[8 : n1 - 8], high], axis=0)
 
     def field(f):
         if f < 3:
@@ -159,16 +201,6 @@
         pack(f, lambda i: ref[1 + i, rows], count, p)
         send(f, 2)
 
-    for pos, k in enumerate((2, 1, 0)):
-        loads[2 * pos].wait()
-        loads[2 * pos + 1].wait()
-        for i in range(n0):
-            inv = 1.0 / D[k, i]
-            D[k, i] = inv
-            S[k, 1 + i, rows] = R[k, i] * inv
-
-    pl.semaphore_wait(barrier, total)
-
     def one(f, a):
         ref, count = field(f)
         if a == 1:
@@ -177,9 +209,16 @@
             pack(f, lambda i: ref[1 + i, rows], count, 2)
         send(f, a)
 
-    one(1, 1)
-    one(2, 2)
-    one(0, 0)
+    for pos, (k, a) in enumerate(((1, 1), (2, 2), (0, 0))):
+        loads[2 * pos].wait()
+        loads[2 * pos + 1].wait()
+        for i in range(n0):
+            inv = 1.0 / D[k, i]
+            D[k, i] = inv
+            S[k, 1 + i, rows] = R[k, i] * inv
+        if pos == 0:
+            pl.semaphore_wait(barrier, total)
+        one(k, a)
     for f, a in ((0, 1), (2, 1), (1, 0), (2, 0), (0, 2), (1, 2)):
         one(f, a)
 
@@ -199,42 +238,48 @@
     for i in range(m0):
         CI[i] = exact(spread_rows, exact(1.0 / (6.0 + CS[i]), spread_cols))
 
+    for i in range(n0):
+        x1, x2 = S[1, 1 + i, rows], S[2, 1 + i, rows]
+        rhs = jnp.where(row_full >= 1, S[1, 1 + i, pl.ds(PAD - 1, n1)], 0.0) - x1
+        rhs = rhs + (jnp.where(lane_full >= 1, pltpu.roll(x2, 1, 1), 0.0) - x2)
+        rhs = rhs - S[0, 1 + i, rows]
+        if i > 0:
+            rhs = rhs + S[0, i, rows]
+        F[0, i] = rhs
     receive(1, 1)
-    rows_x(1, 1)
     receive(0, 0)
     receive(2, 2)
-    ws = arrived(2, 2)
-    for i in range(n0):
-        x2 = S[2, 1 + i, rows]
-        rhs = S[0, i, rows] - S[0, 1 + i, rows]
-        rhs = rhs + (S[1, 1 + i, pl.ds(PAD - 1, n1)] - S[1, 1 + i, rows])
-        rhs = rhs + (from_low(x2, halo(ws, i, 2)) - x2)
-        FG[1 + i, rows] = rhs * NI[i]
+    ws = edges(2, 2)
+    for i in range(n0):
+        rhs = F[0, i] + jnp.where(lane_full < 1, halo(ws, i, 2), 0.0)
+        if i == 0:
+            rhs = rhs + S[0, 0, rows]
+        first = rhs[0:8] + jnp.where(row8 < 1, RX[1, 0, i : i + 1], 0.0)
+        FG[1 + i, rows] = jnp.concatenate([first, rhs[8:]], axis=0) * NI[i]
     exchange(FGI, 2)
 
     def smooth(k):
         for a in range(3):
             if (k, a) not in ((1, 1), (0, 0), (2, 2)):
                 receive(k, a)
-        if k != 1:
-            rows_x(k, 1)
+        rows_x(k, 1)
         w = arrived(k, 2)
         for i in range(n0):
             x = S[k, 1 + i, rows]
             near = S[k, i, rows] + S[k, i + 2, rows] + inplane(S.at[k, 1 + i], x, halo(w, i, 2), 1)
             OB[k, i] = x + near * D[k, i]
 
+    for i in range(n0):
+        F[0, i] = local_near(FG, i, n0, 1)
     smooth(0)
 
     for a in range(3):
         receive(FGI, a)
-    rows_x(FGI, 1)
-    ws = arrived(FGI, 2)
+    ws = edges(FGI, 2)
     for c in range(m0):
         t = None
         for i in (2 * c, 2 * c + 1):
-            x = FG[1 + i, rows]
-            near = FG[i, rows] + FG[i + 2, rows] + inplane(FG.at[1 + i], x, halo(ws, i, 2), 1)
+            near = outer_near(F[0, i], FG, FGI, ws, i, n0, 2)
             F[0, i] = near
             t = near if t is None else t + near
         t = t + jnp.where(lane_full % 2 == 0, pltpu.roll(t, n2 - 1, 1), pltpu.roll(t, 1, 1))
@@ -243,6 +288,8 @@
         CR[c] = t
         V1[1 + c, rows] = t * CI[c]
     exchange(V1I, 4)
+    for c in range(m0):
+        A1[c] = local_near(V1, c, m0, 2)
 
     def faces_f(j):
         f = F0I + j
@@ -259,13 +306,11 @@
 
     for a in range(3):
         receive(V1I, a)
-    rows_x(V1I, 2)
-    ws1 = arrived(V1I, 4)
+    ws = edges(V1I, 4)
     for c in range(m0):
-        x = V1[1 + c, rows]
-        near = V1[c, rows] + V1[c + 2, rows] + inplane(V1.at[1 + c], x, halo(ws1, c, 4), 2)
+        near = outer_near(A1[c], V1, V1I, ws, c, m0, 4)
         A1[c] = CR[c] - near
-        V2[1 + c, rows] = x - near * CI[c]
+        V2[1 + c, rows] = V1[1 + c, rows] - near * CI[c]
     exchange(V2I, 4)
 
     def fold(x):
@@ -289,58 +334,60 @@
         sums[1] = sums[1] + fold(v2 * cr)
         sums[2] = sums[2] + fold(v1 * a1)
         sums[3] = sums[3] + fold(v2 * a1)
-    spread_near(1, V1, ws1)
+        sums[4] = sums[4] + fold(v2 * (a1 - local_near(V2, c, m0, 2)))
+    rows_x(V1I, 2)
+    spread_near(1, V1, arrived(V1I, 4))
 
     for a in range(3):
         receive(V2I, a)
-    rows_x(V2I, 2)
-    ws2 = arrived(V2I, 4)
-    for c in range(m0):
-        x = V2[1 + c, rows]
-        near = V2[c, rows] + V2[c + 2, rows] + inplane(V2.at[1 + c], x, halo(ws2, c, 4), 2)
-        sums[4] = sums[4] + fold(x * (A1[c] - near))
+    outer = fold(V2[1, rows] * V2[0, rows] + V2[m0, rows] * V2[m0 + 1, rows])
+    for v, w in enumerate(edges(V2I, 4)):
+        outer = outer + SY[V2I, v] * w
+    rim = SX[V2I, 0, 0:m0] * RX[V2I, 0, 0:m0] + SX[V2I, 1, 0:m0] * RX[V2I, 1, 0:m0]
+    sums[4] = sums[4] - outer
+    rim = 2.0 * jnp.sum(rim, axis=0, keepdims=True)
+    sums[4] = sums[4] - jnp.where(row8 == 0, rim, 0.0)
     part = jnp.concatenate(
         [jnp.sum(s, axis=0, keepdims=True) for s in sums] + [jnp.zeros((3, n2), jnp.float32)], axis=0
     )
 
-    bases = (0, sizes[0], sizes[0] + sizes[1])
-
-    def sum_message(a, slots, d):
+    def slot(axes, at):
+        index = 0
+        for a in axes:
+            index = index * sizes[a] + at(a)
+        return index
+
+    def sum_message(p, offs, sign):
+        axes, slots = PHASES[p], (PA, PB)[p]
+        other = partner(axes, offs, sign)
+        index = slot(axes, (lambda a: me[a]) if sign > 0 else (lambda a: other[AXES[a]]))
+        sem = p * PA.shape[0] + slot(axes, lambda a: offs[axes.index(a)])
         return pltpu.make_async_remote_copy(
-            src_ref=slots.at[me[a]], dst_ref=slots.at[me[a]],
-            send_sem=psend.at[bases[a] + d], recv_sem=precv.at[bases[a] + d],
-            device_id={AXES[a]: lax.rem(me[a] + d, sizes[a])}, device_id_type=MESH,
+            src_ref=slots.at[index], dst_ref=slots.at[index], send_sem=psend.at[sem], recv_sem=precv.at[sem],
+            device_id=other, device_id_type=MESH,
         )
 
-    def sum_start(a, slots, value):
-        slots[me[a]] = value
-        for d in range(1, sizes[a]):
-            sum_message(a, slots, d).start()
-
-    def sum_end(a, slots):
-        for d in range(1, sizes[a]):
-            src = lax.rem(me[a] + sizes[a] - d, sizes[a])
-            pltpu.make_async_remote_copy(
-                src_ref=slots.at[src], dst_ref=slots.at[src],
-                send_sem=psend.at[bases[a] + d], recv_sem=precv.at[bases[a] + d],
-                device_id={AXES[a]: src}, device_id_type=MESH,
-            ).wait_recv()
-        value = slots[0]
-        for d in range(1, sizes[a]):
-            value = value + slots[d]
-        return value
-
-    sum_start(0, PZ, part)
-    part = sum_end(0, PZ)
-    sum_start(1, PX, part)
-    spread_near(2, V2, ws2)
-    part = sum_end(1, PX)
-    sum_start(2, PY, part)
+    def sum_start(p, value):
+        (PA, PB)[p][slot(PHASES[p], lambda a: me[a])] = value
+        for offs in offsets(PHASES[p]):
+            sum_message(p, offs, 1).start()
+
+    def sum_end(p):
+        for offs in offsets(PHASES[p]):
+            sum_message(p, offs, -1).wait_recv()
+        slots = (PA, PB)[p]
+        return functools.reduce(lambda x, y: x + y, [slots[d] for d in range(slots.shape[0])])
+
+    sum_start(0, part)
+    rows_x(V2I, 2)
+    spread_near(2, V2, arrived(V2I, 4))
+    part = sum_end(0)
+    sum_start(1, part)
     smooth(2)
     for j in range(3):
         for a in range(3):
             receive(F0I + j, a)
-    part = sum_end(2, PY)
+    part = sum_end(1)
     tot = jnp.sum(part, axis=1, keepdims=True)
     gone, gtwo, hone, hmix, htwo = [tot[q : q + 1] for q in range(5)]
     two = (gtwo - hmix * gone / hone) / (htwo - hmix * hmix / hone)
@@ -355,23 +402,15 @@
     for i in range(n0):
         FN[i, n1 : n1 + 1] = mix(lambda j: RX[F0I + j, 1, i : i + 1])
     wf = [mix(lambda j: RY[F0I + j, 1, v]) for v in range(RY.shape[2])]
-    stores = []
     for i in range(n0):
         x = FN[i, 0:n1]
         OB[0, i] = OB[0, i] + (FN[i + 1, 0:n1] - x)
         OB[1, i] = OB[1, i] + (FN[i, 1 : n1 + 1] - x)
         OB[2, i] = OB[2, i] + (from_high(x, halo(wf, i, 2)) - x)
-        if i % 4 == 3 or i == n0 - 1:
-            lo = 4 * (i // 4)
-            for k in range(3):
-                part_of = pl.ds(lo, i + 1 - lo)
-                copy = pltpu.make_async_copy(OB.at[k, part_of], out.at[k, part_of], out_sem.at[len(stores)])
-                copy.start()
-                stores.append(copy)
-
-    for a, slots in ((0, PZ), (1, PX), (2, PY)):
-        for d in range(1, sizes[a]):
-            sum_message(a, slots, d).wait_send()
+
+    for p in (0, 1):
+        for offs in offsets(PHASES[p]):
+            sum_message(p, offs, 1).wait_send()
     for a in range(3):
         for d in (0, 1):
             def drain(a=a, d=d):
@@ -379,8 +418,6 @@
                     if d in dirs(f):
                         message(f, a, d).wait_send()
             pl.when(can_send(a, d))(drain)
-    for copy in stores:
-        copy.wait()
 
 
 def solution(mesh):
@@ -391,26 +428,28 @@
         m0, m1, m2 = coarse_shift.shape
         vecs = max(-(-(n0 * (n1 // 8)) // (n2 // 2)), -(-(m0 * (n1 // 8)) // (n2 // 4)))
         f32 = jnp.float32
+        counts = [math.prod(sizes[a] for a in axes) for axes in PHASES]
         V = lambda *s: pltpu.VMEM(s, f32)
         scratch = [
             V(3, n0, n1, n2), V(3, n0, n1, n2), V(n0, n1, n2), V(m0, m1, m2),
             V(3, n0 + 2, n1 + 2 * PAD, n2), V(n0 + 2, n1 + 2 * PAD, n2),
             V(m0, n1, n2), V(m0, n1, n2), V(m0, n1, n2), V(m0, n1 + 2 * PAD, n2),
             V(m0 + 2, n1 + 2 * PAD, n2), V(m0 + 2, n1 + 2 * PAD, n2),
-            V(3, n0 + 1, n1, n2), V(n0 + 1, n1 + PAD, n2), V(3, n0, n1, n2),
+            V(3, n0 + 1, n1, n2), V(n0 + 1, n1 + PAD, n2),
             V(9, 2, n0, n2), V(9, 2, n0, n2), V(9, vecs, 8, n2), V(9, 2, vecs, 8, n2),
-            V(sizes[0], 8, n2), V(sizes[1], 8, n2), V(sizes[2], 8, n2),
-            pltpu.SemaphoreType.DMA((8,)), pltpu.SemaphoreType.DMA((3 * (-(-n0 // 4)),)),
+            *[V(c, 8, n2) for c in counts],
+            pltpu.SemaphoreType.DMA((8,)),
             pltpu.SemaphoreType.DMA((9, 3, 2)), pltpu.SemaphoreType.DMA((9, 3, 2)),
-            pltpu.SemaphoreType.DMA((sum(sizes),)), pltpu.SemaphoreType.DMA((sum(sizes),)),
+            pltpu.SemaphoreType.DMA((sum(counts),)), pltpu.SemaphoreType.DMA((sum(counts),)),
         ]
+        limit = 67_043_328 - 4 * math.prod(residual.shape) - 2**16
         return pl.pallas_call(
             functools.partial(kernel, sizes),
-            out_shape=jax.ShapeDtypeStruct(residual.shape, f32),
-            in_specs=[pl.BlockSpec(memory_space=pl.ANY)] * 4,
-            out_specs=pl.BlockSpec(memory_space=pl.ANY),
+            out_shape=pltpu.VMEM(residual.shape, f32),
+            in_specs=[pl.BlockSpec(memory_space=pltpu.HBM)] * 4,
+            out_specs=pl.BlockSpec(memory_space=pltpu.VMEM),
             scratch_shapes=scratch,
-            compiler_params=pltpu.CompilerParams(collective_id=0, has_side_effects=True),
+            compiler_params=pltpu.CompilerParams(collective_id=0, has_side_effects=True, vmem_limit_bytes=limit),
         )(residual, edge_diag, node_shift, coarse_shift)
 
     placed = (

time: 33.7 us -> 28.4 us (0.84)
  Pallas kernels: 30.8 us -> 27.1 us
  local copies, waits for them, and re-layouts: 2.73 us -> 1.15 us
    pallas_call x1, Pallas kernels: 30.8 us -> 27.1 us  [local(): pl.pallas_call(functools.partial(kernel, sizes), out_shape=pltpu.VMEM(res...]
    unnamed x1, local copies, waits for them, and re-layouts: 2.73 us -> 1.15 us
where the time goes in v2:
time: 28.4 us; the launch traced here: 28.3 us
  Pallas kernels  27.1 us (95%)
  local copies, waits for them, and re-layouts  1.15 us (4%)
    pallas_call x1, Pallas kernels, local(): pl.pallas_call(functools.partial(kernel, sizes), out_shape=pltpu.VMEM(res...  27.1 us
    unnamed x1, local copies, waits for them, and re-layouts  1.15 us

profile of v2, /device:TPU:0, one launch (start us, length us, event | category | flops | bytes accessed | tf_op | source)
XLA Modules:
  0.0 28.3 jit_solution(958583430755544673)
XLA Ops:
  0.0 27.1 %shard_map.46 = f32[3,16,64,128]{3,2,1,0:T(8,128)S(1)} custom-call(f32[3,16,64,128]{3,2,1,0:T(8,128)} %res.1, f32[3,16,64,128]{3,2,1,0:T(8,128)} %dia.1, f32[16,64,128]{2,1,0:T(8,128)} %shf.1, f32[8,32,64]{2,1,0:T(8,128)} %csh.1), custom_call_target="tpu_custom_call" | custom-call | tf_op jit(solution)/shard_map/pallas_call | solution.py:446
  27.1 1.1 %copy.6 = f32[3,16,64,128]{3,2,1,0:T(8,128)} copy(f32[3,16,64,128]{3,2,1,0:T(8,128)S(1)} %shard_map.46) | data formatting | bytes 3145728

commit v3 on v2

--- a/solution.py
+++ b/solution.py
@@ -13,7 +13,7 @@
 AXES = ("gz", "gx", "gy")
 FGI, V1I, V2I, F0I = 3, 4, 5, 6
 PAD = 8
-PHASES = ((0, 1), (2,))
+PHASES = ((1, 2), (0,))
 
 
 def kernel(
@@ -381,9 +381,9 @@
     sum_start(0, part)
     rows_x(V2I, 2)
     spread_near(2, V2, arrived(V2I, 4))
+    smooth(2)
     part = sum_end(0)
     sum_start(1, part)
-    smooth(2)
     for j in range(3):
         for a in range(3):
             receive(F0I + j, a)

time: 28.4 us -> 27.9 us (0.982)
  the two profiles are of different devices: /device:TPU:0 before, /device:TPU:1 now
where the time goes in v3:
time: 27.9 us; the launch traced here: 27.8 us
  Pallas kernels  26.6 us (95%)
  local copies, waits for them, and re-layouts  1.15 us (4%)
    pallas_call x1, Pallas kernels, local(): pl.pallas_call(functools.partial(kernel, sizes), out_shape=pltpu.VMEM(res...  26.6 us
    unnamed x1, local copies, waits for them, and re-layouts  1.15 us

profile of v3, /device:TPU:1, one launch (start us, length us, event | category | flops | bytes accessed | tf_op | source)
XLA Modules:
  0.0 27.8 jit_solution(6827979562007463765)
XLA Ops:
  0.0 26.6 %shard_map.46 = f32[3,16,64,128]{3,2,1,0:T(8,128)S(1)} custom-call(f32[3,16,64,128]{3,2,1,0:T(8,128)} %res.1, f32[3,16,64,128]{3,2,1,0:T(8,128)} %dia.1, f32[16,64,128]{2,1,0:T(8,128)} %shf.1, f32[8,32,64]{2,1,0:T(8,128)} %csh.1), custom_call_target="tpu_custom_call" | custom-call | tf_op jit(solution)/shard_map/pallas_call | solution.py:446
  26.7 1.1 %copy.6 = f32[3,16,64,128]{3,2,1,0:T(8,128)} copy(f32[3,16,64,128]{3,2,1,0:T(8,128)S(1)} %shard_map.46) | data formatting | bytes 3145728
